TPU v7x, 32 devices: a whole 2x2x4 slice. The times are simulated.
32 devices in a mesh: dp: 8 (over z, x), mp: 4 (over y, core).
Axes of the slice: x: 2, y: 2, z: 4, core: 2. Of those that a mesh axis runs over, the one named last changes fastest.
Arguments:
- acts: bfloat16 [6144, 4, 1984], P('dp', 'mp'), may hold values from -6 to 6
- grads: bfloat16 [6144, 4, 1984], P('dp', 'mp'), may hold values from -0.21875 to 0.21875
- error: bfloat16 [8, 4, 1984, 1984], P('dp', 'mp'), may hold values from -4 to 4
- momentum: float32 [4, 1984, 1984], P('mp', 'dp'), may hold values from -4 to 4
- q_start: float32 [4, 1984, 128], P('mp'), may hold values from -0.125 to 0.125
Outputs:
- error_next: bfloat16 [8, 4, 1984, 1984], P('dp', 'mp')
- momentum_next: float32 [4, 1984, 1984], P('mp', 'dp')
- q_next: float32 [4, 1984, 128], P('mp')
All inputs are finite; a program needn't handle non-finite values.
Results may differ from a plain program's by a relative error of at most 0.001.
Values sent between devices are 32-bit elements; how exact they have to be, the bound alone decides.
No kernel may reach another device: no remote copies, remote signals or barrier semaphores. Data moves between devices by JAX's collectives and lax.ppermute only.
A program may use at most 128 MiB of HBM per device.

v0:
```python
import jax
import jax.numpy as jnp
from jax import lax
from jax.sharding import PartitionSpec as P

D = 3968
PRECISE = lax.Precision.HIGHEST


def per_device(acts, grads, error, momentum, q_start):
    inputs = acts[:, 0, :]
    upstream = grads[:, 0, :]
    local_grad = lax.dot_general(
        inputs, upstream, (((0,), (0,)), ((), ())), preferred_element_type=jnp.float32
    )
    merged = local_grad + error[0, 0].astype(jnp.float32)
    warm_start = q_start[0]
    replicas = lax.axis_size("dp")
    owned_rows = momentum.shape[1]
    left_local = jnp.dot(merged, warm_start, precision=PRECISE)
    left_full = lax.psum(left_local, "dp")
    gram_matrix = jnp.dot(left_full.T, left_full, precision=PRECISE)
    cholesky_low = jnp.linalg.cholesky(gram_matrix)
    ortho_basis = lax.linalg.triangular_solve(
        cholesky_low, left_full, left_side=False, lower=True, transpose_a=True
    )
    basis_owned = lax.dynamic_slice_in_dim(
        ortho_basis, lax.axis_index("dp") * owned_rows, owned_rows, 0
    )
    right_local = lax.dot_general(merged, ortho_basis, (((0,), (0,)), ((), ())), precision=PRECISE)
    q_tile = lax.psum(right_local, "dp") / replicas
    norm_total = lax.psum(jnp.sum(q_tile * q_tile), "mp")
    rms_value = jnp.sqrt(norm_total / (D * D))
    decoded = jnp.dot(ortho_basis, q_tile.T, precision=PRECISE)
    error_next = (merged - decoded).astype(jnp.bfloat16)
    update = jnp.dot(basis_owned, q_tile.T, precision=PRECISE)
    momentum_next = 0.9 * momentum[0] + 0.1 * update / (rms_value + 1e-06)
    return (error_next[None, None], momentum_next[None], q_tile[None])


def solution(mesh):
    in_specs = (
        P("dp", "mp", None),
        P("dp", "mp", None),
        P("dp", "mp", None, None),
        P("mp", "dp", None),
        P("mp", None, None),
    )
    out_specs = (P("dp", "mp", None, None), P("mp", "dp", None), P("mp", None, None))
    return jax.shard_map(
        per_device, mesh=mesh, in_specs=in_specs, out_specs=out_specs, check_vma=False
    )
```

profile of v0, /device:TPU:0, one launch (start us, length us, event | category | flops | bytes accessed | tf_op | source)
XLA Modules:
  0.0 297.2 jit_solution(10708653032430564272)
XLA Ops:
  7.2 0.0 copy-start
  7.2 0.0 all-reduce.3.cloned.1.call-start
  7.2 1.8 copy-done
  9.0 9.3 %convert_add_fusion = f32[1984,1984]{1,0:T(8,128)S(1)} fusion(bf16[1,1,1984,1984]{3,2,1,0:T(8,128)(2,1)} %param.7, bf16[768,1,1984]{0,2,1:T(8,128)(2,1)S(1)} %copy-done, bf16[768,1,1984]{0,2,1:T(8,128)(2,1)} %param.5), kind=kOutput, calls=%fused_computation | convolution fusion | flops 6053961728 | bytes 29712384 | tf_op jit(solution)/shard_map/dot_general | solution.py:13
  18.4 5.6 %copy-done.1 = f32[1984,1984]{1,0:T(8,128)} copy-done((f32[1984,1984]{1,0:T(8,128)}, f32[1984,1984]{1,0:T(8,128)S(1)}, u32[]{:S(2)}) %copy-start.1) | copy-done | bytes 15745048
  24.0 15.3 %fusion.6 = f32[1984,128]{1,0:T(8,128)} fusion(f32[1984,1984]{1,0:T(8,128)S(1)} %convert_add_fusion, f32[1,1984,128]{2,1,0:T(8,128)} %param.9), kind=kOutput, calls=%fused_computation.9 | convolution fusion | flops 6046089216 | bytes 17776640 | tf_op jit(solution)/shard_map/dot_general | solution.py:20
  39.3 0.0 all-reduce.3.cloned.1.call-update
  39.3 0.2 all-reduce.5.cloned.1.call-start
  39.6 80.8 %all-reduce.3.cloned.1.call-done = f32[1984,128]{1,0:T(8,128)} async-done(((f32[1984,128]{1,0:T(8,128)}), f32[1984,128]{1,0:T(8,128)}) %all-reduce.3.cloned.1.call-update) | async-done | bytes 1015824 | tf_op jit(solution)/shard_map/psum | solution.py:21
  120.3 3.3 %fusion.20 = f32[128,128]{1,0:T(8,128)S(1)} fusion(f32[1984,128]{1,0:T(8,128)} %all-reduce.3.cloned.1.call-done), kind=kOutput, calls=%fused_computation.31 | convolution fusion | flops 390070272 | bytes 1081344 | tf_op jit(solution)/shard_map/dot_general | solution.py:22
  123.7 0.1 copy.8
  123.8 11.7 %cholesky.16 = f32[128,128]{1,0:T(8,128)S(1)} custom-call(f32[128,128]{1,0:T(8,128)S(1)} %fusion.16), custom_call_target="Cholesky" | custom-call | tf_op jit(solution)/shard_map/jit(cholesky)/cholesky | solution.py:23
  135.5 0.6 compare_reduce_fusion
  136.2 0.7 fusion.13
  136.9 9.8 %custom-call.6 = f32[1,128,128]{1,2,0:T(8,128)S(1)} custom-call(f32[1,128,128]{2,1,0:T(8,128)S(1)} %fusion.13), custom_call_target="InvertDiagBlocksLowerTriangular" | custom-call | tf_op jit(solution)/shard_map/triangular_solve | solution.py:24
  146.7 2.2 fusion.14
  148.8 1.0 copy-done.2
  149.8 29.9 %fusion.21 = f32[1984,128]{1,0:T(8,128)} fusion(f32[1984,1984]{1,0:T(8,128)} %copy-done.1, f32[1984,128]{1,0:T(8,128)S(1)} %fusion.14), kind=kOutput, calls=%fused_computation.32 | convolution fusion | flops 6046089216 | bytes 17776640 | tf_op jit(solution)/shard_map/dot_general | solution.py:30
  179.7 0.0 all-reduce.5.cloned.1.call-update
  179.7 77.0 %all-reduce.5.cloned.1.call-done = f32[1984,128]{1,0:T(8,128)} async-done(((f32[1984,128]{1,0:T(8,128)}), f32[1984,128]{1,0:T(8,128)}) %all-reduce.5.cloned.1.call-update) | async-done | bytes 1015824 | tf_op jit(solution)/shard_map/psum | solution.py:31
  256.8 3.0 multiply_bitcast_fusion
  259.7 6.5 %psum.23 = f32[]{:T(128)} all-reduce(f32[]{:T(128)} %get-tuple-element.4), channel_id=1, replica_groups=mesh['dp'=8,'mp'=4] {'mp'}, use_global_device_ids=true, to_apply=%region_5.6 | all-reduce | flops 1 | bytes 8 | tf_op jit(solution)/shard_map/psum | solution.py:32
  267.0 19.2 %fusion = bf16[1,1,1984,1984]{3,2,1,0:T(8,128)(2,1)} fusion(f32[1984,1984]{1,0:T(8,128)} %copy-done.1, f32[1984,128]{1,0:T(8,128)} %copy-done.2, f32[1984,128]{1,0:T(8,128)} %all-reduce.5.cloned.1.call-done), kind=kOutput, calls=%fused_computation.2 | convolution fusion | flops 6054215680 | bytes 25649152 | tf_op jit(solution)/shard_map/dot_general | solution.py:34
  286.1 4.2 %fusion.5 = f32[1,248,1984]{2,1,0:T(8,128)} fusion(f32[1,248,1984]{2,1,0:T(8,128)S(1)} %copy-done.4, f32[]{:T(128)S(6)} %add.32, f32[1984,128]{1,0:T(8,128)S(1)} %copy-done.3, f32[1984,128]{1,0:T(8,128)} %copy-done.2, s32[]{:T(128)S(6)} %select_n.8), kind=kOutput, calls=%fused_computation.8 | convolution fusion | flops 757983232 | bytes 5079048 | tf_op jit(solution)/shard_map/dot_general | solution.py:36
  (8 shorter events, 0.1 us)
Async XLA Ops:
  7.2 1.9 copy-start
  7.2 113.1 %all-reduce.3.cloned.1.call-start = ((), (), s32[]{:S(2)}) async-start(), calls=%async_computation | async-start | bytes 2031616 | tf_op jit(solution)/shard_map/psum | solution.py:21
  18.4 5.6 %copy-start.1 = (f32[1984,1984]{1,0:T(8,128)}, f32[1984,1984]{1,0:T(8,128)S(1)}, u32[]{:S(2)}) copy-start(f32[1984,1984]{1,0:T(8,128)S(1)} %convert_add_fusion) | copy-start | bytes 47235076
  39.3 217.4 %all-reduce.5.cloned.1.call-start = ((), (), s32[]{:S(2)}) async-start(), calls=%async_computation.1 | async-start | bytes 2031616 | tf_op jit(solution)/shard_map/psum | solution.py:31
  148.8 1.0 copy-start.2
  266.9 19.2 %copy-start.3 = (f32[1984,128]{1,0:T(8,128)S(1)}, f32[1984,128]{1,0:T(8,128)}, u32[]{:S(2)}) copy-start(f32[1984,128]{1,0:T(8,128)} %all-reduce.5.cloned.1.call-done) | copy-start | bytes 3047428
  267.0 19.2 %copy-start.4 = (f32[1,248,1984]{2,1,0:T(8,128)S(1)}, f32[1,248,1984]{2,1,0:T(8,128)}, u32[]{:S(2)}) copy-start(f32[1,248,1984]{2,1,0:T(8,128)} %param.8) | copy-start | bytes 5904388
Sparse Core Ops, SparseCore 0:
  39.4 80.8 all-reduce.2
  179.8 76.8 all-reduce.4
where the time goes:
time: 298 us; the launch traced here: 297 us
  waiting for transfers between devices  158 us (53%)
  matrix products  83.4 us (28%)
  other arithmetic  25.8 us (9%)
  between operations  14.8 us (5%)
  local copies, waits for them, and re-layouts  8.49 us (3%)
  blocking collectives  6.53 us (2%)
    psum x1, waiting for transfers between devices, per_device(): left_full = lax.psum(left_local, 'dp')  80.8 us
    psum x1, waiting for transfers between devices, per_device(): q_tile = lax.psum(right_local, 'dp') / replicas  77 us
    dot_general x1, matrix products, per_device(): lax.dot_general(merged, ortho_basis, (((0,), (0,)), ((), ())), precision=...  29.9 us
    dot_general x1, matrix products, per_device(): decoded = jnp.dot(ortho_basis, q_tile.T, precision=PRECISE)  19.2 us
    dot_general x1, matrix products, per_device(): left_local = jnp.dot(merged, warm_start, precision=PRECISE)  15.3 us
    another operation x3, other arithmetic, per_device(): cholesky_low = jnp.linalg.cholesky(gram_matrix)  12.4 us
    another operation x2, other arithmetic, per_device(): lax.linalg.triangular_solve(cholesky_low, left_full, left_side=False, low...  10.5 us
    dot_general x1, matrix products, per_device(): lax.dot_general(inputs, upstream, (((0,), (0,)), ((), ())), preferred_ele...  9.34 us
  transfers between devices with their start and end apart: 2, of which 2 were waited for; matrix products, arithmetic and copies ran while one was open for 0% of the time, Pallas kernels for 0%

commit v1 on v0

--- a/solution.py
+++ b/solution.py
@@ -18,7 +18,18 @@
     replicas = lax.axis_size("dp")
     owned_rows = momentum.shape[1]
     left_local = jnp.dot(merged, warm_start, precision=PRECISE)
-    left_full = lax.psum(left_local, "dp")
+
+    def name_core_all(inner_x, chip_axis):
+        k_all = lax.axis_size(chip_axis)
+        value_now = inner_x
+        for tick in [
+            [(idx, idx ^ q) for idx in range(k_all)] for q in (1, 2, 4, 8, 16) if q < k_all
+        ]:
+            latest = lax.ppermute(value_now, chip_axis, tick)
+            value_now = value_now + latest
+        return value_now
+
+    left_full = name_core_all(left_local, "dp")
     gram_matrix = jnp.dot(left_full.T, left_full, precision=PRECISE)
     cholesky_low = jnp.linalg.cholesky(gram_matrix)
     ortho_basis = lax.linalg.triangular_solve(

time: 298 us -> 308 us (1.034)
  waiting for transfers between devices: 158 us -> 166 us
  starting transfers between devices: 0.26 us -> 7.56 us
  local copies, waits for them, and re-layouts: 8.49 us -> 3.83 us
    ppermute x0 -> x3, waiting for transfers between devices: none -> 87.1 us  [name_core_all(): latest = lax.ppermute(value_now, chip_axis, tick)]
    psum x1 -> x0, waiting for transfers between devices: 80.8 us -> none  [per_device(): left_full = lax.psum(left_local, 'dp')]
    ppermute x0 -> x3, starting transfers between devices: none -> 7.52 us  [name_core_all(): latest = lax.ppermute(value_now, chip_axis, tick)]
    unnamed x10 -> x12, local copies, waits for them, and re-layouts: 8.4 us -> 3.74 us
  transfers between devices with their start and end apart: 2 -> 4, of which waited for: 2 -> 4; matrix products, arithmetic and copies ran while one was open for 0% -> 0% of each run, Pallas kernels for 0% -> 0%
where the time goes in v1:
time: 308 us; the launch traced here: 307 us
  waiting for transfers between devices  166 us (54%)
  matrix products  82.4 us (27%)
  other arithmetic  26.1 us (8%)
  between operations  14.9 us (5%)
  starting transfers between devices  7.56 us (2%)
  blocking collectives  6.53 us (2%)
  local copies, waits for them, and re-layouts  3.83 us (1%)
    ppermute x3, waiting for transfers between devices, name_core_all(): latest = lax.ppermute(value_now, chip_axis, tick)  87.1 us
    psum x1, waiting for transfers between devices, per_device(): q_tile = lax.psum(right_local, 'dp') / replicas  79 us
    dot_general x1, matrix products, per_device(): lax.dot_general(merged, ortho_basis, (((0,), (0,)), ((), ())), precision=...  29.9 us
    dot_general x1, matrix products, per_device(): decoded = jnp.dot(ortho_basis, q_tile.T, precision=PRECISE)  19.2 us
    dot_general x1, matrix products, per_device(): left_local = jnp.dot(merged, warm_start, precision=PRECISE)  15.8 us
    another operation x3, other arithmetic, per_device(): cholesky_low = jnp.linalg.cholesky(gram_matrix)  12.4 us
    another operation x2, other arithmetic, per_device(): lax.linalg.triangular_solve(cholesky_low, left_full, left_side=False, low...  10.5 us
    dot_general x1, matrix products, per_device(): lax.dot_general(inputs, upstream, (((0,), (0,)), ((), ())), preferred_ele...  9.34 us
  transfers between devices with their start and end apart: 4, of which 4 were waited for; matrix products, arithmetic and copies ran while one was open for 0% of the time, Pallas kernels for 0%

profile of v1, /device:TPU:0, one launch (start us, length us, event | category | flops | bytes accessed | tf_op | source)
XLA Modules:
  0.0 307.5 jit_solution(16255628074430396967)
XLA Ops:
  7.2 1.8 copy-done
  9.0 9.3 %convert_add_fusion = f32[1984,1984]{1,0:T(8,128)S(1)} fusion(bf16[1,1,1984,1984]{3,2,1,0:T(8,128)(2,1)} %param.7, bf16[768,1,1984]{0,2,1:T(8,128)(2,1)S(1)} %copy-done, bf16[768,1,1984]{0,2,1:T(8,128)(2,1)} %param.5), kind=kOutput, calls=%fused_computation | convolution fusion | flops 6053961728 | bytes 29712384 | tf_op jit(solution)/shard_map/dot_general | solution.py:13
  18.4 15.8 %fusion.6 = f32[1984,128]{1,0:T(8,128)S(1)} fusion(f32[1984,1984]{1,0:T(8,128)S(1)} %convert_add_fusion, f32[1,1984,128]{2,1,0:T(8,128)} %param.9), kind=kOutput, calls=%fused_computation.9 | convolution fusion | flops 6046089216 | bytes 17776640 | tf_op jit(solution)/shard_map/dot_general | solution.py:20
  34.2 3.0 collective-permute-start
  37.2 22.5 %collective-permute-done = f32[1984,128]{1,0:T(8,128)S(1)} collective-permute-done((f32[1984,128]{1,0:T(8,128)S(1)}, f32[1984,128]{1,0:T(8,128)S(1)}, u32[]{:S(2)}, u32[]{:S(2)}) %collective-permute-start) | collective-permute-done | bytes 1015840 | tf_op jit(solution)/shard_map/ppermute | solution.py:28
  59.7 0.1 add.37
  59.8 1.9 collective-permute-start.1
  61.7 21.8 %collective-permute-done.1 = f32[1984,128]{1,0:T(8,128)S(1)} collective-permute-done((f32[1984,128]{1,0:T(8,128)S(1)}, f32[1984,128]{1,0:T(8,128)S(1)}, u32[]{:S(2)}, u32[]{:S(2)}) %collective-permute-start.1) | collective-permute-done | bytes 1015840 | tf_op jit(solution)/shard_map/ppermute | solution.py:28
  83.6 2.6 collective-permute-start.2
  86.2 42.9 %collective-permute-done.2 = f32[1984,128]{1,0:T(8,128)S(1)} collective-permute-done((f32[1984,128]{1,0:T(8,128)S(1)}, f32[1984,128]{1,0:T(8,128)S(1)}, u32[]{:S(2)}, u32[]{:S(2)}) %collective-permute-start.2) | collective-permute-done | bytes 1015840 | tf_op jit(solution)/shard_map/ppermute | solution.py:28
  129.2 0.9 copy-done.2
  130.1 1.8 fusion.20
  132.1 11.7 %cholesky.16 = f32[128,128]{1,0:T(8,128)S(1)} custom-call(f32[128,128]{1,0:T(8,128)S(1)} %fusion.16), custom_call_target="Cholesky" | custom-call | tf_op jit(solution)/shard_map/jit(cholesky)/cholesky | solution.py:34
  143.8 0.6 compare_reduce_fusion
  144.5 0.7 fusion.13
  145.1 9.8 %custom-call.6 = f32[1,128,128]{1,2,0:T(8,128)S(1)} custom-call(f32[1,128,128]{2,1,0:T(8,128)S(1)} %fusion.13), custom_call_target="InvertDiagBlocksLowerTriangular" | custom-call | tf_op jit(solution)/shard_map/triangular_solve | solution.py:35
  155.0 2.2 fusion.14
  157.1 1.0 copy-done.3
  158.1 29.9 %fusion.21 = f32[1984,128]{1,0:T(8,128)} fusion(f32[1984,1984]{1,0:T(8,128)} %copy-done.1, f32[1984,128]{1,0:T(8,128)S(1)} %fusion.14), kind=kOutput, calls=%fused_computation.32 | convolution fusion | flops 6046089216 | bytes 17776640 | tf_op jit(solution)/shard_map/dot_general | solution.py:41
  188.0 79.0 %all-reduce.2.cloned.1.call-done = f32[1984,128]{1,0:T(8,128)} async-done(((f32[1984,128]{1,0:T(8,128)}), f32[1984,128]{1,0:T(8,128)}) %all-reduce.2.cloned.1.call-update) | async-done | bytes 1015824 | tf_op jit(solution)/shard_map/psum | solution.py:42
  267.0 3.0 multiply_bitcast_fusion
  270.0 6.5 %psum.15 = f32[]{:T(128)} all-reduce(f32[]{:T(128)} %get-tuple-element.4), channel_id=1, replica_groups=mesh['dp'=8,'mp'=4] {'mp'}, use_global_device_ids=true, to_apply=%region_4.5 | all-reduce | flops 1 | bytes 8 | tf_op jit(solution)/shard_map/psum | solution.py:43
  277.2 19.2 %fusion = bf16[1,1,1984,1984]{3,2,1,0:T(8,128)(2,1)} fusion(f32[1984,1984]{1,0:T(8,128)} %copy-done.1, f32[1984,128]{1,0:T(8,128)} %copy-done.3, f32[1984,128]{1,0:T(8,128)} %all-reduce.2.cloned.1.call-done), kind=kOutput, calls=%fused_computation.2 | convolution fusion | flops 6054215680 | bytes 25649152 | tf_op jit(solution)/shard_map/dot_general | solution.py:45
  296.4 4.2 %fusion.5 = f32[1,248,1984]{2,1,0:T(8,128)} fusion(f32[1,248,1984]{2,1,0:T(8,128)S(1)} %copy-done.5, f32[]{:T(128)S(6)} %add.42, f32[1984,128]{1,0:T(8,128)S(1)} %copy-done.4, f32[1984,128]{1,0:T(8,128)} %copy-done.3, s32[]{:T(128)S(6)} %select_n.8), kind=kOutput, calls=%fused_computation.8 | convolution fusion | flops 757983232 | bytes 5079048 | tf_op jit(solution)/shard_map/dot_general | solution.py:47
  (16 shorter events, 0.4 us)
Async XLA Ops:
  7.2 1.9 copy-start
  7.2 259.9 %all-reduce.2.cloned.1.call-start = ((), (), s32[]{:S(2)}) async-start(), calls=%async_computation | async-start | bytes 2031616 | tf_op jit(solution)/shard_map/psum | solution.py:42
  18.4 15.8 %copy-start.1 = (f32[1984,1984]{1,0:T(8,128)}, f32[1984,1984]{1,0:T(8,128)S(1)}, u32[]{:S(2)}) copy-start(f32[1984,1984]{1,0:T(8,128)S(1)} %convert_add_fusion) | copy-start | bytes 47235076
  34.2 25.5 %collective-permute-start = (f32[1984,128]{1,0:T(8,128)S(1)}, f32[1984,128]{1,0:T(8,128)S(1)}, u32[]{:S(2)}, u32[]{:S(2)}) collective-permute-start(f32[1984,128]{1,0:T(8,128)S(1)} %fusion.6), channel_id=1, source_target_pairs={{0,4},{4,0},{8,12},{12,8},{16,20},{20,16},{24,28},{28,24},{1,5},{5... | collective-permute-start | bytes 3047432 | tf_op jit(solution)/shard_map/ppermute | solution.py:28
  59.8 23.7 %collective-permute-start.1 = (f32[1984,128]{1,0:T(8,128)S(1)}, f32[1984,128]{1,0:T(8,128)S(1)}, u32[]{:S(2)}, u32[]{:S(2)}) collective-permute-start(f32[1984,128]{1,0:T(8,128)S(1)} %add.37), channel_id=1, source_target_pairs={{0,8},{4,12},{8,0},{12,4},{16,24},{20,28},{24,16},{28,20},{1,9},{5... | collective-permute-start | bytes 3047432 | tf_op jit(solution)/shard_map/ppermute | solution.py:28
  83.6 45.5 %collective-permute-start.2 = (f32[1984,128]{1,0:T(8,128)S(1)}, f32[1984,128]{1,0:T(8,128)S(1)}, u32[]{:S(2)}, u32[]{:S(2)}) collective-permute-start(f32[1984,128]{1,0:T(8,128)S(1)} %add.38), channel_id=1, source_target_pairs={{0,16},{4,20},{8,24},{12,28},{16,0},{20,4},{24,8},{28,12},{1,17},{... | collective-permute-start | bytes 3047432 | tf_op jit(solution)/shard_map/ppermute | solution.py:28
  129.2 1.0 copy-start.2
  157.1 1.0 copy-start.3
  277.2 19.2 %copy-start.4 = (f32[1984,128]{1,0:T(8,128)S(1)}, f32[1984,128]{1,0:T(8,128)}, u32[]{:S(2)}) copy-start(f32[1984,128]{1,0:T(8,128)} %all-reduce.2.cloned.1.call-done) | copy-start | bytes 3047428
  277.2 19.2 %copy-start.5 = (f32[1,248,1984]{2,1,0:T(8,128)S(1)}, f32[1,248,1984]{2,1,0:T(8,128)}, u32[]{:S(2)}) copy-start(f32[1,248,1984]{2,1,0:T(8,128)} %param.8) | copy-start | bytes 5904388
Sparse Core Ops, SparseCore 0:
  188.1 78.8 all-reduce.1
